TPU v7x, 32 devices: a whole 2x2x4 slice. The times are simulated.
32 devices in a mesh: rep: 8 (over y, x, core), tp: 4 (over z).
Axes of the slice: x: 2, y: 2, z: 4, core: 2. Of those that a mesh axis runs over, the one named last changes fastest.
Arguments:
- tokens: bfloat16 [8192, 1280], P(('rep', 'tp')), may hold values from -6 to 6
- view_ids: int32 [32, 4], P('rep'), may hold values from 0 to 31
- time_ids: int32 [32], P('rep'), may hold values from 0 to 999
- camera_table: float32 [32, 1280], replicated, may hold values from -6 to 6
- norm_attn: float32 [2, 1280], replicated, may hold values from 0.1 to 1.9
- norm_ffn: float32 [2, 1280], replicated, may hold values from 0.1 to 1.9
- w_query: bfloat16 [2, 1280, 1280], P(None, ('rep', 'tp')), may hold values from -0.1677051 to 0.1677051
- w_key: bfloat16 [2, 1280, 1280], P(None, ('rep', 'tp')), may hold values from -6.764106 to 6.764106
- w_value: bfloat16 [2, 1280, 1280], P(None, ('rep', 'tp')), may hold values from -0.15625 to 0.15625
- w_out: bfloat16 [2, 1280, 1280], P(None, ('rep', 'tp')), may hold values from -0.15625 to 0.15625
- w_gate: bfloat16 [2, 1280, 5120], P(None, ('rep', 'tp')), may hold values from -0.15625 to 0.15625
- w_up: bfloat16 [2, 1280, 5120], P(None, ('rep', 'tp')), may hold values from -0.15625 to 0.15625
- w_down: bfloat16 [2, 1280, 5120], P(None, ('rep', 'tp')), may hold values from -0.078125 to 0.078125
Outputs:
- denoised: bfloat16 [8192, 1280], P(('rep', 'tp'))
All inputs are finite; a program needn't handle non-finite values.
Results may differ from a plain program's by a relative error of at most 0.035.
Values may be sent and summed in bfloat16 or wider, within the bound.
A program may use at most 128 MiB of HBM per device.

v0:
```python
import math
import jax
import jax.numpy as jnp
from jax import lax
from jax.sharding import PartitionSpec as P

D = 1280
HEADS = 8
VIEWS = 4
HW = 64
LAYERS = 2


def layer_norm(activations, gain_vector):
    average = jnp.mean(activations, axis=-1, keepdims=True)
    centred = activations - average
    spread = jnp.mean(centred * centred, axis=-1, keepdims=True)
    return (centred * lax.rsqrt(spread + 1e-05) * gain_vector).astype(jnp.bfloat16)


def time_code(step_ids, width):
    half_width = width // 2
    frequency = jnp.exp(-math.log(10000.0) * jnp.arange(half_width, dtype=jnp.float32) / half_width)
    angles = step_ids.astype(jnp.float32)[:, None] * frequency[None, :]
    return jnp.concatenate([jnp.cos(angles), jnp.sin(angles)], axis=1)


def conditioning(row_ids, view_ids, time_ids, camera_table):
    set_ids = row_ids // (VIEWS * HW)
    slot_ids = set_ids * VIEWS + row_ids // HW % VIEWS
    flat_views = view_ids.reshape(-1)
    slot_range = jnp.arange(flat_views.shape[0], dtype=jnp.int32)
    pose_ids = jnp.sum(
        jnp.where(slot_ids[:, None] == slot_range[None, :], flat_views[None, :], 0), axis=1
    )
    set_range = jnp.arange(time_ids.shape[0], dtype=jnp.int32)
    step_ids = jnp.sum(
        jnp.where(set_ids[:, None] == set_range[None, :], time_ids[None, :], 0), axis=1
    )
    pose_range = jnp.arange(camera_table.shape[0], dtype=jnp.int32)
    onehot_pose = (pose_ids[:, None] == pose_range[None, :]).astype(jnp.float32)
    camera = jnp.dot(onehot_pose, camera_table, precision=lax.Precision.HIGHEST)
    return camera + time_code(step_ids, camera_table.shape[1])


def reshard(weights):
    owned = (
        lax.all_to_all(weights[0], "tp", split_axis=2, concat_axis=1, tiled=True),
        lax.all_to_all(weights[1], "tp", split_axis=2, concat_axis=1, tiled=True),
        lax.all_to_all(weights[2], "tp", split_axis=2, concat_axis=1, tiled=True),
        lax.all_to_all(weights[3], "tp", split_axis=2, concat_axis=1, tiled=True),
        lax.all_to_all(weights[4], "tp", split_axis=2, concat_axis=1, tiled=True),
        lax.all_to_all(weights[5], "tp", split_axis=2, concat_axis=1, tiled=True),
        lax.all_to_all(weights[6], "tp", split_axis=2, concat_axis=1, tiled=True),
    )
    return (
        lax.all_gather(owned[0], "rep", axis=1, tiled=True),
        lax.all_gather(owned[1], "rep", axis=1, tiled=True),
        lax.all_gather(owned[2], "rep", axis=1, tiled=True),
        lax.all_gather(owned[3], "rep", axis=1, tiled=True),
        lax.all_gather(owned[4], "rep", axis=1, tiled=True),
        lax.all_gather(owned[5], "rep", axis=1, tiled=True),
        lax.all_gather(owned[6], "rep", axis=1, tiled=True),
    )


def attend(packed, width_local, head_size):
    total_rows = packed.shape[0]
    set_count = total_rows // (VIEWS * HW)
    heads_here = width_local // head_size
    shape_heads = (set_count, VIEWS * HW, heads_here, head_size)
    query_rows = packed[:, :width_local].reshape(shape_heads)
    key_rows = packed[:, width_local : 2 * width_local].reshape(shape_heads)
    value_rows = packed[:, 2 * width_local :].reshape(shape_heads)
    scores = jnp.einsum(
        "bqhd,bkhd->bhqk", query_rows, key_rows, preferred_element_type=jnp.float32
    ) * head_size ** (-0.5)
    peak = jnp.max(scores, axis=-1, keepdims=True)
    expons = jnp.exp(scores - peak)
    attn_probs = (expons / jnp.sum(expons, axis=-1, keepdims=True)).astype(jnp.bfloat16)
    mixed_rows = jnp.einsum(
        "bhqk,bkhd->bqhd", attn_probs, value_rows, preferred_element_type=jnp.float32
    )
    return mixed_rows.astype(jnp.bfloat16).reshape(total_rows, width_local)


def out_terms(mixed_rows, weight):
    return lax.dot_general(
        mixed_rows, weight, (((1,), (1,)), ((), ())), preferred_element_type=jnp.float32
    )


def body(
    tokens,
    view_ids,
    time_ids,
    camera_table,
    norm_attn,
    norm_ffn,
    w_query,
    w_key,
    w_value,
    w_out,
    w_gate,
    w_up,
    w_down,
):
    tp_count = lax.axis_size("tp")
    query_w, key_w, value_w, out_w, gate_w, up_w, down_w = reshard(
        (w_query, w_key, w_value, w_out, w_gate, w_up, w_down)
    )
    width_local = query_w.shape[2]
    head_size = D // HEADS
    share_rows = tokens.shape[0]
    group_total = share_rows * tp_count
    first_row = lax.axis_index("tp") * share_rows
    whole_rows = lax.all_gather(tokens, "tp", axis=0, tiled=True)
    row_ids = jnp.arange(group_total, dtype=jnp.int32)
    stream = whole_rows.astype(jnp.float32) + conditioning(
        row_ids, view_ids, time_ids, camera_table
    )

    def total_terms(partial_value):
        return lax.psum(partial_value.astype(jnp.bfloat16), "tp").astype(jnp.float32)

    for layer_index in range(LAYERS):
        query_here = query_w[layer_index]
        key_here = key_w[layer_index]
        value_here = value_w[layer_index]
        gate_here = gate_w[layer_index]
        up_here = up_w[layer_index]
        normed = layer_norm(stream, norm_attn[layer_index])
        packed = jnp.concatenate(
            [
                jnp.dot(normed, query_here, preferred_element_type=jnp.float32).astype(
                    jnp.bfloat16
                ),
                jnp.dot(normed, key_here, preferred_element_type=jnp.float32).astype(jnp.bfloat16),
                jnp.dot(normed, value_here, preferred_element_type=jnp.float32).astype(
                    jnp.bfloat16
                ),
            ],
            axis=1,
        )
        mixed_rows = attend(packed, width_local, head_size)
        stream = stream + total_terms(out_terms(mixed_rows, out_w[layer_index]))
        normed = layer_norm(stream, norm_ffn[layer_index])
        gate_part = jnp.dot(normed, gate_here, preferred_element_type=jnp.float32)
        up_part = jnp.dot(normed, up_here, preferred_element_type=jnp.float32)
        hidden = (jax.nn.gelu(gate_part, approximate=False) * up_part).astype(jnp.bfloat16)
        stream = stream + total_terms(out_terms(hidden, down_w[layer_index]))
    return lax.dynamic_slice_in_dim(stream, first_row, share_rows, 0).astype(jnp.bfloat16)


def solution(mesh):
    return jax.shard_map(
        body,
        mesh=mesh,
        in_specs=(
            P(("rep", "tp"), None),
            P("rep", None),
            P("rep"),
            P(),
            P(),
            P(),
            P(None, ("rep", "tp"), None),
            P(None, ("rep", "tp"), None),
            P(None, ("rep", "tp"), None),
            P(None, ("rep", "tp"), None),
            P(None, ("rep", "tp"), None),
            P(None, ("rep", "tp"), None),
            P(None, ("rep", "tp"), None),
        ),
        out_specs=P(("rep", "tp"), None),
        check_vma=False,
    )
```

profile of v0, /device:TPU:0, one launch (start us, length us, event | category | flops | bytes accessed | tf_op | source)
XLA Modules:
  0.0 892.5 jit_solution(10918619393631502398)
XLA Ops:
  9.8 13.8 %all_to_all.126 = bf16[4,2,12800]{2,1,0:T(2,128)(2,1)S(1)} all-to-all(bf16[4,2,12800]{2,1,0:T(2,128)(2,1)S(1)} %reshape.139), channel_id=1, replica_groups=mesh['rep'=8,'tp'=4] {'tp'}, dimensions={0} | all-to-all | bytes 409600 | tf_op jit(solution)/shard_map/all_to_all | solution.py:48
  27.8 19.7 %all_to_all.127 = bf16[4,2,12800]{2,1,0:T(2,128)(2,1)S(1)} all-to-all(bf16[4,2,12800]{2,1,0:T(2,128)(2,1)S(1)} %reshape.137), channel_id=1, replica_groups=mesh['rep'=8,'tp'=4] {'tp'}, dimensions={0} | all-to-all | bytes 409600 | tf_op jit(solution)/shard_map/all_to_all | solution.py:49
  51.7 14.9 %all_to_all.128 = bf16[4,2,12800]{2,1,0:T(2,128)(2,1)S(1)} all-to-all(bf16[4,2,12800]{2,1,0:T(2,128)(2,1)S(1)} %reshape.141), channel_id=1, replica_groups=mesh['rep'=8,'tp'=4] {'tp'}, dimensions={0} | all-to-all | bytes 409600 | tf_op jit(solution)/shard_map/all_to_all | solution.py:50
  75.7 10.5 %multiply_cosine_fusion = (f32[1024,640]{1,0:T(8,128)S(1)}, f32[1024,640]{1,0:T(8,128)}) fusion(f32[640]{0:T(1024)S(1)} %multiply_exponential_fusion, f32[1024]{0:T(1024)S(1)} %convert_element_type.93), kind=kLoop, calls=%fused_computation.60 | loop fusion | flops 655360 | bytes 5249536 | tf_op jit(solution)/shard_map/cos | solution.py:25
  91.8 5.1 fusion.139
  100.0 4.8 all-gather.13.cloned.1.call-done
  109.7 24.3 %all-gather.15.cloned.1.call-done = bf16[2,1280,320]{2,1,0:T(8,128)(2,1)} async-done(((bf16[2,160,320]{2,1,0:T(8,128)(2,1)}), bf16[2,1280,320]{2,1,0:T(8,128)(2,1)}) %all-gather.15.cloned.1.call-update) | async-done | bytes 1638416 | tf_op jit(solution)/shard_map/all_gather | solution.py:58
  139.5 23.4 %all-gather.11.cloned.1.call-done = bf16[2,1280,320]{2,1,0:T(8,128)(2,1)} async-done(((bf16[2,160,320]{2,1,0:T(8,128)(2,1)}), bf16[2,1280,320]{2,1,0:T(8,128)(2,1)}) %all-gather.11.cloned.1.call-update) | async-done | bytes 1638416 | tf_op jit(solution)/shard_map/all_gather | solution.py:59
  173.8 18.1 %all-gather.17.cloned.1.call-done = bf16[2,1280,320]{2,1,0:T(8,128)(2,1)} async-done(((bf16[2,160,320]{2,1,0:T(8,128)(2,1)}), bf16[2,1280,320]{2,1,0:T(8,128)(2,1)}) %all-gather.17.cloned.1.call-update) | async-done | bytes 1638416 | tf_op jit(solution)/shard_map/all_gather | solution.py:60
  192.0 4.3 convolution_convert_fusion.3
  196.6 4.7 copy.97
  201.3 5.1 reshape.145
  206.4 47.9 %all_to_all.129 = bf16[4,2,51200]{2,1,0:T(2,128)(2,1)} all-to-all(bf16[4,2,51200]{2,1,0:T(2,128)(2,1)} %reshape.145), channel_id=1, replica_groups=mesh['rep'=8,'tp'=4] {'tp'}, dimensions={0} | all-to-all | bytes 1638400 | tf_op jit(solution)/shard_map/all_to_all | solution.py:52
  254.2 5.0 reshape.146
  259.3 4.3 copy.117
  265.8 4.7 copy.100
  270.6 5.1 reshape.147
  275.6 47.5 %all_to_all.130 = bf16[4,2,51200]{2,1,0:T(2,128)(2,1)} all-to-all(bf16[4,2,51200]{2,1,0:T(2,128)(2,1)} %reshape.147), channel_id=1, replica_groups=mesh['rep'=8,'tp'=4] {'tp'}, dimensions={0} | all-to-all | bytes 1638400 | tf_op jit(solution)/shard_map/all_to_all | solution.py:53
  323.2 5.0 reshape.148
  334.7 4.7 copy.103
  339.4 5.1 reshape.135
  344.5 25.6 %all_to_all.131 = bf16[4,2,51200]{2,1,0:T(2,128)(2,1)} all-to-all(bf16[4,2,51200]{2,1,0:T(2,128)(2,1)} %reshape.135), channel_id=1, replica_groups=mesh['rep'=8,'tp'=4] {'tp'}, dimensions={0} | all-to-all | bytes 1638400 | tf_op jit(solution)/shard_map/all_to_all | solution.py:54
  370.2 5.0 reshape.136
  392.4 8.8 fusion.26
  401.2 29.3 %all-gather.21.cloned.1.call-done = bf16[2,1280,1280]{2,1,0:T(8,128)(2,1)} async-done(((bf16[2,160,1280]{2,1,0:T(8,128)(2,1)}), bf16[2,1280,1280]{2,1,0:T(8,128)(2,1)}) %all-gather.21.cloned.1.call-update) | async-done | bytes 6553616 | tf_op jit(solution)/shard_map/all_gather | solution.py:62
  430.5 48.4 %all-gather.23.cloned.1.call-done = bf16[2,1280,1280]{2,1,0:T(8,128)(2,1)} async-done(((bf16[2,160,1280]{2,1,0:T(8,128)(2,1)}), bf16[2,1280,1280]{2,1,0:T(8,128)(2,1)}) %all-gather.23.cloned.1.call-update) | async-done | bytes 6553616 | tf_op jit(solution)/shard_map/all_gather | solution.py:63
  478.9 23.3 %convolution_convert_fusion.2 = bf16[1024,1280]{1,0:T(8,128)(2,1)} fusion(bf16[2,1280,1280]{2,1,0:T(8,128)(2,1)} %all-gather.23.cloned.1.call-done, f32[1024,1280]{1,0:T(8,128)} %fusion.26, bf16[1024,1280]{1,0:T(8,128)(2,1)} %multiply_convert_fusion.2, bf16[2,1280,1280]{2,1,0:T(8,128)(2,1)} %all-gather.21.cloned.1.call-done), kind=kOutput, calls=%fused_computation.57 | convolution fusion | flops 6798704640 | bytes 17039360 | tf_op jit(solution)/shard_map/dot_general | solution.py:88
  502.3 104.2 %all-reduce.7.cloned.1.call-done = bf16[1024,1280]{1,0:T(8,128)(2,1)} async-done(((bf16[1024,1280]{1,0:T(8,128)(2,1)}), bf16[1024,1280]{1,0:T(8,128)(2,1)}) %all-reduce.7.cloned.1.call-update) | async-done | bytes 2621456 | tf_op jit(solution)/shard_map/psum | solution.py:124
  637.8 103.2 %all-reduce.9.cloned.1.call-done = bf16[1024,1280]{1,0:T(8,128)(2,1)} async-done(((bf16[1024,1280]{1,0:T(8,128)(2,1)}), bf16[1024,1280]{1,0:T(8,128)(2,1)}) %all-reduce.9.cloned.1.call-update) | async-done | bytes 2621456 | tf_op jit(solution)/shard_map/psum | solution.py:124
  747.2 7.9 fusion.25
  755.1 24.4 %convolution_convert_fusion = bf16[1024,1280]{1,0:T(8,128)(2,1)} fusion(bf16[2,1280,1280]{2,1,0:T(8,128)(2,1)} %all-gather.23.cloned.1.call-done, f32[1024,1280]{1,0:T(8,128)} %fusion.25, bf16[2,1280,1280]{2,1,0:T(8,128)(2,1)} %all-gather.21.cloned.1.call-done, f32[1024,1280]{1,0:T(8,128)} %copy-done.5, f32[1280]{0:T(1024)S(1)} %get-tuple-element.5, ...), kind=kOutput, calls=%fused_computation.55 | convolution fusion | flops 6803947520 | bytes 19674112 | tf_op jit(solution)/shard_map/dot_general | solution.py:88
  779.4 103.2 %all-reduce.11.cloned.1.call-done = bf16[1024,1280]{1,0:T(8,128)(2,1)} async-done(((bf16[1024,1280]{1,0:T(8,128)(2,1)}), bf16[1024,1280]{1,0:T(8,128)(2,1)}) %all-reduce.11.cloned.1.call-update) | async-done | bytes 2621456 | tf_op jit(solution)/shard_map/psum | solution.py:124
  (138 shorter events, 116.2 us)
Async XLA Ops:
  6.5 85.3 %copy-start = (f32[32,1280]{1,0:T(8,128)S(1)}, f32[32,1280]{1,0:T(8,128)}, u32[]{:S(2)}) copy-start(f32[32,1280]{1,0:T(8,128)} %param.16) | copy-start | bytes 491524
  6.5 19.6 %copy-start.6 = (bf16[2,40,1280]{2,1,0:T(8,128)(2,1)S(1)}, bf16[2,40,1280]{2,1,0:T(8,128)(2,1)}, u32[]{:S(2)}) copy-start(bf16[2,40,1280]{2,1,0:T(8,128)(2,1)} %param.20) | copy-start | bytes 614404
  6.5 43.5 %copy-start.7 = (bf16[2,40,1280]{2,1,0:T(8,128)(2,1)S(1)}, bf16[2,40,1280]{2,1,0:T(8,128)(2,1)}, u32[]{:S(2)}) copy-start(bf16[2,40,1280]{2,1,0:T(8,128)(2,1)} %param.21) | copy-start | bytes 614404
  6.5 85.3 %all-gather.9.cloned.1.call-start = ((), (), s32[]{:S(2)}) async-start(), calls=%async_computation.7 | async-start | bytes 3276800 | tf_op jit(solution)/shard_map/all_gather | solution.py:117
  7.3 97.5 %all-gather.13.cloned.1.call-start = ((), (), s32[]{:S(2)}) async-start(), calls=%async_computation.9 | async-start | bytes 2211840 | tf_op jit(solution)/shard_map/all_gather | solution.py:57
  24.6 44.4 %copy-start.8 = (bf16[2,40,1280]{2,1,0:T(8,128)(2,1)S(1)}, bf16[2,40,1280]{2,1,0:T(8,128)(2,1)}, u32[]{:S(2)}) copy-start(bf16[2,40,1280]{2,1,0:T(8,128)(2,1)} %param.22) | copy-start | bytes 614404
  26.1 107.8 %all-gather.15.cloned.1.call-start = ((), (), s32[]{:S(2)}) async-start(), calls=%async_computation.10 | async-start | bytes 2211840 | tf_op jit(solution)/shard_map/all_gather | solution.py:58
  26.7 48.7 %copy-start.12 = (s32[4]{0:T(128)S(1)}, s32[4]{0:T(128)}, u32[]{:S(2)}) copy-start(s32[4]{0:T(128)} %param.15) | copy-start | bytes 52
  26.7 48.8 %copy-start.11 = (s32[4,4]{1,0:T(4,128)S(1)}, s32[4,4]{1,0:T(4,128)}, u32[]{:S(2)}) copy-start(s32[4,4]{1,0:T(4,128)} %param.14) | copy-start | bytes 196
  26.7 48.9 %copy-start.9 = (f32[2,1280]{1,0:T(2,128)S(1)}, f32[2,1280]{1,0:T(2,128)}, u32[]{:S(2)}) copy-start(f32[2,1280]{1,0:T(2,128)} %param.17) | copy-start | bytes 30724
  50.0 112.9 %all-gather.11.cloned.1.call-start = ((), (), s32[]{:S(2)}) async-start(), calls=%async_computation.8 | async-start | bytes 2211840 | tf_op jit(solution)/shard_map/all_gather | solution.py:59
  71.3 15.0 %all-to-all-start.3 = ((bf16[4,2,12800]{2,1,0:T(2,128)(2,1)}), bf16[4,2,12800]{2,1,0:T(2,128)(2,1)}, u32[]{:S(2)}, u32[]{:S(2)}) async-start(bf16[4,2,12800]{2,1,0:T(2,128)(2,1)} %reshape.143), calls=%async_computation.3 | async-start | bytes 409600 | tf_op jit(solution)/shard_map/all_to_all | solution.py:51
  75.3 116.7 %all-gather.17.cloned.1.call-start = ((), (), s32[]{:S(2)}) async-start(), calls=%async_computation.11 | async-start | bytes 2211840 | tf_op jit(solution)/shard_map/all_gather | solution.py:60
  91.6 290.2 %all-reduce.5.cloned.1.call-start = ((), (), s32[]{:S(2)}) async-start(), calls=%async_computation.12 | async-start | bytes 5242880 | tf_op jit(solution)/shard_map/psum | solution.py:124
  97.0 2.3 copy-start.2
  196.3 196.1 %all-gather.19.cloned.1.call-start = ((), (), s32[]{:S(2)}) async-start(), calls=%async_computation.13 | async-start | bytes 7372800 | tf_op jit(solution)/shard_map/all_gather | solution.py:61
  265.8 164.7 %all-gather.21.cloned.1.call-start = ((), (), s32[]{:S(2)}) async-start(), calls=%async_computation.14 | async-start | bytes 7372800 | tf_op jit(solution)/shard_map/all_gather | solution.py:62
  334.7 144.3 %all-gather.23.cloned.1.call-start = ((), (), s32[]{:S(2)}) async-start(), calls=%async_computation.15 | async-start | bytes 7372800 | tf_op jit(solution)/shard_map/all_gather | solution.py:63
  344.5 37.2 %copy-start.10 = (f32[2,1280]{1,0:T(2,128)S(1)}, f32[2,1280]{1,0:T(2,128)}, u32[]{:S(2)}) copy-start(f32[2,1280]{1,0:T(2,128)} %param.18) | copy-start | bytes 30724
  381.6 224.9 %all-reduce.7.cloned.1.call-start = ((), (), s32[]{:S(2)}) async-start(), calls=%async_computation.16 | async-start | bytes 5242880 | tf_op jit(solution)/shard_map/psum | solution.py:124
  381.8 4.1 copy-start.4
  381.8 7.7 slice-start
  385.8 3.7 slice-start.1
  502.3 238.7 %all-reduce.9.cloned.1.call-start = ((), (), s32[]{:S(2)}) async-start(), calls=%async_computation.17 | async-start | bytes 5242880 | tf_op jit(solution)/shard_map/psum | solution.py:124
  610.7 2.3 copy-start.3
  611.4 2.7 copy-start.13
  631.8 2.7 copy-start.14
  637.8 244.9 %all-reduce.11.cloned.1.call-start = ((), (), s32[]{:S(2)}) async-start(), calls=%async_computation.18 | async-start | bytes 5242880 | tf_op jit(solution)/shard_map/psum | solution.py:124
  744.9 2.3 copy-start.5
  755.0 130.1 %copy-start.1 = (f32[32,1280]{1,0:T(8,128)S(1)}, f32[32,1280]{1,0:T(8,128)}, u32[]{:S(2)}) copy-start(f32[32,1280]{1,0:T(8,128)} %param.16) | copy-start | bytes 491524
Sparse Core Ops, SparseCore 0:
  8.9 66.1 all-gather.8
  77.0 27.7 all-gather.12
  106.7 27.2 all-gather.14
  135.7 27.2 all-gather.10
  164.7 27.2 all-gather.16
  196.4 138.2 all-reduce.4
  336.6 45.3 all-gather.18
  384.0 46.4 all-gather.20
  432.4 46.4 all-gather.22
  502.4 104.0 all-reduce.6
  637.9 103.0 all-reduce.8
  779.6 103.0 all-reduce.10
where the time goes:
time: 902 us; the launch traced here: 892 us
  waiting for transfers between devices  460 us (51%)
  blocking collectives  169 us (19%)
  matrix products  105 us (12%)
  local copies, waits for them, and re-layouts  103 us (11%)
  other arithmetic  35.2 us (4%)
  between operations  14.7 us (2%)
    psum x4, waiting for transfers between devices, total_terms(): lax.psum(partial_value.astype(jnp.bfloat16), 'tp').astype(jnp.float32)  311 us
    unnamed x57, local copies, waits for them, and re-layouts  62.7 us
    dot_general x4, matrix products, out_terms(): lax.dot_general(mixed_rows, weight, (((1,), (1,)), ((), ())), preferred_e...  55.2 us
    all_gather x1, waiting for transfers between devices, reshard(): lax.all_gather(owned[6], 'rep', axis=1, tiled=True)  48.4 us
    all_to_all x1, blocking collectives, reshard(): lax.all_to_all(weights[4], 'tp', split_axis=2, concat_axis=1, tiled=True)  47.9 us
    all_to_all x1, blocking collectives, reshard(): lax.all_to_all(weights[5], 'tp', split_axis=2, concat_axis=1, tiled=True)  47.5 us
    all_gather x1, waiting for transfers between devices, reshard(): lax.all_gather(owned[5], 'rep', axis=1, tiled=True)  29.3 us
    all_to_all x1, blocking collectives, reshard(): lax.all_to_all(weights[6], 'tp', split_axis=2, concat_axis=1, tiled=True)  25.6 us
  transfers between devices with their start and end apart: 13, of which 9 were waited for; matrix products, arithmetic and copies ran while one was open for 16% of the time, Pallas kernels for 0%

commit v1 on v0

--- a/solution.py
+++ b/solution.py
@@ -9,6 +9,12 @@
 VIEWS = 4
 HW = 64
 LAYERS = 2
+
+
+def stack_and_merge(block, axis, dim):
+    parts = lax.all_gather(block, axis, axis=0, tiled=False)
+    result = jnp.concatenate(parts, axis=dim)
+    return result
 
 
 def layer_norm(activations, gain_vector):
@@ -60,7 +66,7 @@
         lax.all_gather(owned[3], "rep", axis=1, tiled=True),
         lax.all_gather(owned[4], "rep", axis=1, tiled=True),
         lax.all_gather(owned[5], "rep", axis=1, tiled=True),
-        lax.all_gather(owned[6], "rep", axis=1, tiled=True),
+        stack_and_merge(owned[6], "rep", 1),
     )
 
 

time: 902 us -> 899 us (level)
    all_to_all x1, blocking collectives: 25.6 us -> 47.5 us  [reshard(): lax.all_to_all(weights[6], 'tp', split_axis=2, concat_axis=1, tiled=True)]
    all_to_all x1, blocking collectives: 47.5 us -> 25.7 us  [reshard(): lax.all_to_all(weights[5], 'tp', split_axis=2, concat_axis=1, tiled=True)]
    all_gather x1, waiting for transfers between devices: 48.4 us -> 29.4 us  [stack_and_merge(): parts = lax.all_gather(block, axis, axis=0, tiled=False)]
    all_gather x1, waiting for transfers between devices: 29.3 us -> 42.4 us  [reshard(): lax.all_gather(owned[5], 'rep', axis=1, tiled=True)]
    unnamed x57 -> x59, local copies, waits for them, and re-layouts: 62.7 us -> 61.2 us
  transfers between devices with their start and end apart: 13 -> 13, of which waited for: 9 -> 9; matrix products, arithmetic and copies ran while one was open for 16% -> 17% of each run, Pallas kernels for 0% -> 0%
where the time goes in v1:
time: 899 us; the launch traced here: 889 us
  waiting for transfers between devices  454 us (51%)
  blocking collectives  169 us (19%)
  local copies, waits for them, and re-layouts  108 us (12%)
  matrix products  103 us (11%)
  other arithmetic  35 us (4%)
  between operations  14.4 us (2%)
    psum x4, waiting for transfers between devices, total_terms(): lax.psum(partial_value.astype(jnp.bfloat16), 'tp').astype(jnp.float32)  311 us
    unnamed x59, local copies, waits for them, and re-layouts  61.2 us
    dot_general x4, matrix products, out_terms(): lax.dot_general(mixed_rows, weight, (((1,), (1,)), ((), ())), preferred_e...  52.3 us
    all_to_all x1, blocking collectives, reshard(): lax.all_to_all(weights[4], 'tp', split_axis=2, concat_axis=1, tiled=True)  47.9 us
    all_to_all x1, blocking collectives, reshard(): lax.all_to_all(weights[6], 'tp', split_axis=2, concat_axis=1, tiled=True)  47.5 us
    all_gather x1, waiting for transfers between devices, reshard(): lax.all_gather(owned[5], 'rep', axis=1, tiled=True)  42.4 us
    all_gather x1, waiting for transfers between devices, stack_and_merge(): parts = lax.all_gather(block, axis, axis=0, tiled=False)  29.4 us
    all_to_all x1, blocking collectives, reshard(): lax.all_to_all(weights[5], 'tp', split_axis=2, concat_axis=1, tiled=True)  25.7 us
  transfers between devices with their start and end apart: 13, of which 9 were waited for; matrix products, arithmetic and copies ran while one was open for 17% of the time, Pallas kernels for 0%

profile of v1, /device:TPU:0, one launch (start us, length us, event | category | flops | bytes accessed | tf_op | source)
XLA Modules:
  0.0 889.0 jit_solution(12029725930016066722)
XLA Ops:
  9.8 13.8 %all_to_all.123 = bf16[4,2,12800]{2,1,0:T(2,128)(2,1)S(1)} all-to-all(bf16[4,2,12800]{2,1,0:T(2,128)(2,1)S(1)} %reshape.149), channel_id=1, replica_groups=mesh['rep'=8,'tp'=4] {'tp'}, dimensions={0} | all-to-all | bytes 409600 | tf_op jit(solution)/shard_map/all_to_all | solution.py:54
  27.8 19.7 %all_to_all.124 = bf16[4,2,12800]{2,1,0:T(2,128)(2,1)S(1)} all-to-all(bf16[4,2,12800]{2,1,0:T(2,128)(2,1)S(1)} %reshape.147), channel_id=1, replica_groups=mesh['rep'=8,'tp'=4] {'tp'}, dimensions={0} | all-to-all | bytes 409600 | tf_op jit(solution)/shard_map/all_to_all | solution.py:55
  51.7 14.8 %all_to_all.125 = bf16[4,2,12800]{2,1,0:T(2,128)(2,1)S(1)} all-to-all(bf16[4,2,12800]{2,1,0:T(2,128)(2,1)S(1)} %reshape.151), channel_id=1, replica_groups=mesh['rep'=8,'tp'=4] {'tp'}, dimensions={0} | all-to-all | bytes 409600 | tf_op jit(solution)/shard_map/all_to_all | solution.py:56
  75.7 10.5 %multiply_cosine_fusion = (f32[1024,640]{1,0:T(8,128)S(1)}, f32[1024,640]{1,0:T(8,128)}) fusion(f32[640]{0:T(1024)S(1)} %multiply_exponential_fusion, f32[1024]{0:T(1024)S(1)} %convert_element_type.93), kind=kLoop, calls=%fused_computation.60 | loop fusion | flops 655360 | bytes 5249536 | tf_op jit(solution)/shard_map/cos | solution.py:31
  92.1 5.1 fusion.140
  100.2 4.6 all-gather.13.cloned.1.call-done
  109.7 24.3 %all-gather.15.cloned.1.call-done = bf16[2,1280,320]{2,1,0:T(8,128)(2,1)} async-done(((bf16[2,160,320]{2,1,0:T(8,128)(2,1)}), bf16[2,1280,320]{2,1,0:T(8,128)(2,1)}) %all-gather.15.cloned.1.call-update) | async-done | bytes 1638416 | tf_op jit(solution)/shard_map/all_gather | solution.py:64
  139.6 23.4 %all-gather.11.cloned.1.call-done = bf16[2,1280,320]{2,1,0:T(8,128)(2,1)} async-done(((bf16[2,160,320]{2,1,0:T(8,128)(2,1)}), bf16[2,1280,320]{2,1,0:T(8,128)(2,1)}) %all-gather.11.cloned.1.call-update) | async-done | bytes 1638416 | tf_op jit(solution)/shard_map/all_gather | solution.py:65
  173.8 18.1 %all-gather.17.cloned.1.call-done = bf16[2,1280,320]{2,1,0:T(8,128)(2,1)} async-done(((bf16[2,160,320]{2,1,0:T(8,128)(2,1)}), bf16[2,1280,320]{2,1,0:T(8,128)(2,1)}) %all-gather.17.cloned.1.call-update) | async-done | bytes 1638416 | tf_op jit(solution)/shard_map/all_gather | solution.py:66
  192.0 4.3 convolution_convert_fusion.3
  196.6 4.7 copy.97
  201.3 5.1 reshape.155
  206.3 47.9 %all_to_all.126 = bf16[4,2,51200]{2,1,0:T(2,128)(2,1)} all-to-all(bf16[4,2,51200]{2,1,0:T(2,128)(2,1)} %reshape.155), channel_id=1, replica_groups=mesh['rep'=8,'tp'=4] {'tp'}, dimensions={0} | all-to-all | bytes 1638400 | tf_op jit(solution)/shard_map/all_to_all | solution.py:58
  254.2 5.0 reshape.156
  265.8 4.7 copy.103
  270.5 5.1 reshape.145
  275.6 47.5 %all_to_all.127 = bf16[4,2,51200]{2,1,0:T(2,128)(2,1)} all-to-all(bf16[4,2,51200]{2,1,0:T(2,128)(2,1)} %reshape.145), channel_id=1, replica_groups=mesh['rep'=8,'tp'=4] {'tp'}, dimensions={0} | all-to-all | bytes 1638400 | tf_op jit(solution)/shard_map/all_to_all | solution.py:60
  323.2 5.0 reshape.146
  334.8 4.7 copy.100
  339.5 5.1 reshape.157
  344.6 25.7 %all_to_all.128 = bf16[4,2,51200]{2,1,0:T(2,128)(2,1)} all-to-all(bf16[4,2,51200]{2,1,0:T(2,128)(2,1)} %reshape.157), channel_id=1, replica_groups=mesh['rep'=8,'tp'=4] {'tp'}, dimensions={0} | all-to-all | bytes 1638400 | tf_op jit(solution)/shard_map/all_to_all | solution.py:59
  370.2 5.0 reshape.158
  392.3 8.8 fusion.26
  401.2 29.4 %all-gather.23.cloned.1.call-done = bf16[8,2,160,1280]{3,2,1,0:T(8,128)(2,1)} async-done(((bf16[1,2,160,1280]{3,2,1,0:T(8,128)(2,1)}), bf16[8,2,160,1280]{3,2,1,0:T(8,128)(2,1)}) %all-gather.23.cloned.1.call-update) | async-done | bytes 6553616 | tf_op jit(solution)/shard_map/all_gather | solution.py:15
  430.5 6.0 fusion.139
  436.6 42.4 %all-gather.21.cloned.1.call-done = bf16[2,1280,1280]{2,1,0:T(8,128)(2,1)} async-done(((bf16[2,160,1280]{2,1,0:T(8,128)(2,1)}), bf16[2,1280,1280]{2,1,0:T(8,128)(2,1)}) %all-gather.21.cloned.1.call-update) | async-done | bytes 6553616 | tf_op jit(solution)/shard_map/all_gather | solution.py:68
  479.0 23.6 %convolution_convert_fusion.2 = bf16[1024,1280]{1,0:T(8,128)(2,1)} fusion(bf16[1280,1280]{1,0:T(8,128)(2,1)} %bitcast.127, f32[1024,1280]{1,0:T(8,128)} %fusion.26, bf16[1024,1280]{1,0:T(8,128)(2,1)} %multiply_convert_fusion.2, bf16[2,1280,1280]{2,1,0:T(8,128)(2,1)} %all-gather.21.cloned.1.call-done), kind=kOutput, calls=%fused_computation.57 | convolution fusion | flops 6798704640 | bytes 17039360 | tf_op jit(solution)/shard_map/dot_general | solution.py:94
  502.6 104.2 %all-reduce.7.cloned.1.call-done = bf16[1024,1280]{1,0:T(8,128)(2,1)} async-done(((bf16[1024,1280]{1,0:T(8,128)(2,1)}), bf16[1024,1280]{1,0:T(8,128)(2,1)}) %all-reduce.7.cloned.1.call-update) | async-done | bytes 2621456 | tf_op jit(solution)/shard_map/psum | solution.py:130
  638.0 103.2 %all-reduce.9.cloned.1.call-done = bf16[1024,1280]{1,0:T(8,128)(2,1)} async-done(((bf16[1024,1280]{1,0:T(8,128)(2,1)}), bf16[1024,1280]{1,0:T(8,128)(2,1)}) %all-reduce.9.cloned.1.call-update) | async-done | bytes 2621456 | tf_op jit(solution)/shard_map/psum | solution.py:130
  745.8 9.1 %fusion.25 = f32[1024,1280]{1,0:T(8,128)} fusion(bf16[2,1280,1280]{2,1,0:T(8,128)(2,1)} %all-gather.19.cloned.1.call-done, f32[1024,1280]{1,0:T(8,128)S(1)} %get-tuple-element.10, f32[1280]{0:T(1024)S(1)} %get-tuple-element.5, f32[1024]{0:T(1024)S(1)} %add_rsqrt_fusion, f32[1024]{0:T(1024)S(1)} %broadcast_multiply_fusion), kind=kOutput, calls=%fused_computation.63 | convolution fusion | flops 3360686080 | bytes 13775872 | tf_op jit(solution)/shard_map/dot_general | solution.py:154
  754.9 21.3 %convolution_convert_fusion = bf16[1024,1280]{1,0:T(8,128)(2,1)} fusion(bf16[1280,1280]{1,0:T(8,128)(2,1)S(1)} %bitcast.126, f32[1024,1280]{1,0:T(8,128)} %fusion.25, bf16[2,1280,1280]{2,1,0:T(8,128)(2,1)} %all-gather.21.cloned.1.call-done, f32[1024,1280]{1,0:T(8,128)} %copy-done.5, f32[1280]{0:T(1024)S(1)} %get-tuple-element.5, ...), kind=kOutput, calls=%fused_computation.55 | convolution fusion | flops 6803947520 | bytes 19674112 | tf_op jit(solution)/shard_map/dot_general | solution.py:94
  776.2 103.2 %all-reduce.11.cloned.1.call-done = bf16[1024,1280]{1,0:T(8,128)(2,1)} async-done(((bf16[1024,1280]{1,0:T(8,128)(2,1)}), bf16[1024,1280]{1,0:T(8,128)(2,1)}) %all-reduce.11.cloned.1.call-update) | async-done | bytes 2621456 | tf_op jit(solution)/shard_map/psum | solution.py:130
  (141 shorter events, 119.0 us)
Async XLA Ops:
  6.5 85.6 %copy-start = (f32[32,1280]{1,0:T(8,128)S(1)}, f32[32,1280]{1,0:T(8,128)}, u32[]{:S(2)}) copy-start(f32[32,1280]{1,0:T(8,128)} %param.16) | copy-start | bytes 491524
  6.5 19.6 %copy-start.7 = (bf16[2,40,1280]{2,1,0:T(8,128)(2,1)S(1)}, bf16[2,40,1280]{2,1,0:T(8,128)(2,1)}, u32[]{:S(2)}) copy-start(bf16[2,40,1280]{2,1,0:T(8,128)(2,1)} %param.20) | copy-start | bytes 614404
  6.5 43.5 %copy-start.8 = (bf16[2,40,1280]{2,1,0:T(8,128)(2,1)S(1)}, bf16[2,40,1280]{2,1,0:T(8,128)(2,1)}, u32[]{:S(2)}) copy-start(bf16[2,40,1280]{2,1,0:T(8,128)(2,1)} %param.21) | copy-start | bytes 614404
  6.5 85.5 %all-gather.9.cloned.1.call-start = ((), (), s32[]{:S(2)}) async-start(), calls=%async_computation.7 | async-start | bytes 3276800 | tf_op jit(solution)/shard_map/all_gather | solution.py:123
  7.3 97.5 %all-gather.13.cloned.1.call-start = ((), (), s32[]{:S(2)}) async-start(), calls=%async_computation.9 | async-start | bytes 2211840 | tf_op jit(solution)/shard_map/all_gather | solution.py:63
  24.6 44.4 %copy-start.9 = (bf16[2,40,1280]{2,1,0:T(8,128)(2,1)S(1)}, bf16[2,40,1280]{2,1,0:T(8,128)(2,1)}, u32[]{:S(2)}) copy-start(bf16[2,40,1280]{2,1,0:T(8,128)(2,1)} %param.22) | copy-start | bytes 614404
  26.1 107.9 %all-gather.15.cloned.1.call-start = ((), (), s32[]{:S(2)}) async-start(), calls=%async_computation.10 | async-start | bytes 2211840 | tf_op jit(solution)/shard_map/all_gather | solution.py:64
  26.7 48.7 %copy-start.13 = (s32[4]{0:T(128)S(1)}, s32[4]{0:T(128)}, u32[]{:S(2)}) copy-start(s32[4]{0:T(128)} %param.15) | copy-start | bytes 52
  26.7 48.8 %copy-start.12 = (s32[4,4]{1,0:T(4,128)S(1)}, s32[4,4]{1,0:T(4,128)}, u32[]{:S(2)}) copy-start(s32[4,4]{1,0:T(4,128)} %param.14) | copy-start | bytes 196
  26.7 48.9 %copy-start.10 = (f32[2,1280]{1,0:T(2,128)S(1)}, f32[2,1280]{1,0:T(2,128)}, u32[]{:S(2)}) copy-start(f32[2,1280]{1,0:T(2,128)} %param.17) | copy-start | bytes 30724
  50.0 113.0 %all-gather.11.cloned.1.call-start = ((), (), s32[]{:S(2)}) async-start(), calls=%async_computation.8 | async-start | bytes 2211840 | tf_op jit(solution)/shard_map/all_gather | solution.py:65
  71.3 14.9 %all-to-all-start.3 = ((bf16[4,2,12800]{2,1,0:T(2,128)(2,1)}), bf16[4,2,12800]{2,1,0:T(2,128)(2,1)}, u32[]{:S(2)}, u32[]{:S(2)}) async-start(bf16[4,2,12800]{2,1,0:T(2,128)(2,1)} %reshape.153), calls=%async_computation.3 | async-start | bytes 409600 | tf_op jit(solution)/shard_map/all_to_all | solution.py:57
  75.3 116.7 %all-gather.17.cloned.1.call-start = ((), (), s32[]{:S(2)}) async-start(), calls=%async_computation.11 | async-start | bytes 2211840 | tf_op jit(solution)/shard_map/all_gather | solution.py:66
  91.6 290.3 %all-reduce.5.cloned.1.call-start = ((), (), s32[]{:S(2)}) async-start(), calls=%async_computation.12 | async-start | bytes 5242880 | tf_op jit(solution)/shard_map/psum | solution.py:130
  97.2 2.3 copy-start.2
  196.3 196.0 %all-gather.19.cloned.1.call-start = ((), (), s32[]{:S(2)}) async-start(), calls=%async_computation.13 | async-start | bytes 7372800 | tf_op jit(solution)/shard_map/all_gather | solution.py:67
  265.7 164.8 %all-gather.23.cloned.1.call-start = ((), (), s32[]{:S(2)}) async-start(), calls=%async_computation.15 | async-start | bytes 7372800 | tf_op jit(solution)/shard_map/all_gather | solution.py:15
  334.7 144.3 %all-gather.21.cloned.1.call-start = ((), (), s32[]{:S(2)}) async-start(), calls=%async_computation.14 | async-start | bytes 7372800 | tf_op jit(solution)/shard_map/all_gather | solution.py:68
  344.6 37.2 %copy-start.11 = (f32[2,1280]{1,0:T(2,128)S(1)}, f32[2,1280]{1,0:T(2,128)}, u32[]{:S(2)}) copy-start(f32[2,1280]{1,0:T(2,128)} %param.18) | copy-start | bytes 30724
  381.8 225.0 %all-reduce.7.cloned.1.call-start = ((), (), s32[]{:S(2)}) async-start(), calls=%async_computation.16 | async-start | bytes 5242880 | tf_op jit(solution)/shard_map/psum | solution.py:130
  381.9 4.1 copy-start.4
  381.9 7.7 slice-start
  386.0 3.7 slice-start.1
  502.6 238.6 %all-reduce.9.cloned.1.call-start = ((), (), s32[]{:S(2)}) async-start(), calls=%async_computation.17 | async-start | bytes 5242880 | tf_op jit(solution)/shard_map/psum | solution.py:130
  611.0 2.3 copy-start.3
  611.7 2.7 copy-start.14
  632.0 2.7 copy-start.15
  637.9 241.6 %all-reduce.11.cloned.1.call-start = ((), (), s32[]{:S(2)}) async-start(), calls=%async_computation.18 | async-start | bytes 5242880 | tf_op jit(solution)/shard_map/psum | solution.py:130
  745.1 9.8 %copy-start.5 = (f32[1024,1280]{1,0:T(8,128)}, f32[1024,1280]{1,0:T(8,128)S(1)}, u32[]{:S(2)}) copy-start(f32[1024,1280]{1,0:T(8,128)S(1)} %get-tuple-element.10) | copy-start | bytes 15728644
  745.8 9.1 %copy-start.6 = (bf16[1,8,160,1280]{3,2,0,1:T(8,128)(2,1)S(1)}, bf16[1,8,160,1280]{3,2,0,1:T(8,128)(2,1)}, u32[]{:S(2)}) copy-start(bf16[1,8,160,1280]{3,2,0,1:T(8,128)(2,1)} %get-tuple-element.13) | copy-start | bytes 9830404
  754.9 127.0 %copy-start.1 = (f32[32,1280]{1,0:T(8,128)S(1)}, f32[32,1280]{1,0:T(8,128)}, u32[]{:S(2)}) copy-start(f32[32,1280]{1,0:T(8,128)} %param.16) | copy-start | bytes 491524
Sparse Core Ops, SparseCore 0:
  8.9 66.1 all-gather.8
  77.0 27.7 all-gather.12
  106.7 27.2 all-gather.14
  135.7 27.2 all-gather.10
  164.7 27.2 all-gather.16
  196.4 138.2 all-reduce.4
  336.7 45.3 all-gather.18
  384.0 46.4 all-gather.22
  432.4 46.4 all-gather.20
  502.7 104.0 all-reduce.6
  638.0 103.0 all-reduce.8
  776.4 103.0 all-reduce.10
